TPU v7x, 32 devices: a whole 2x2x4 slice. The times are simulated.
32 devices in a mesh: grid: 16 (over z, x, core), band: 2 (over y).
Axes of the slice: x: 2, y: 2, z: 4, core: 2. Of those that a mesh axis runs over, the one named last changes fastest.
Arguments:
- states: float32 [4096, 256], P('grid', 'band'), may hold values from -6 to 6
- potential: float32 [4096], P('grid'), may hold values from -3 to 0
- bounds: float32 [3], replicated, may hold values from -9 to 26, as said below
- point_count: int32 [16], P('grid'), may hold values from 128 to 256, as said below
- send_rows: int32 [16, 6, 64], P('grid'), may hold values from 0 to 256
- stencil_table: int32 [36, 4096], P(None, 'grid'), may hold values from 0 to 640, as said below
Outputs:
- filtered: float32 [4096, 256], P('grid', 'band')
- margin: float32 [256, 256], P(('grid', 'band'))
Inputs may be any that keep to these rules, and one draw needn't show every extreme that they name: `point_count`: one partition has exactly 256 live points in every draw; rows at or past a partition's count are padding. A block has a length from half of 64 to 64: below it the entries are live rows of g, from it on they are 256; some block is full in every draw. Blocks to partitions that do not exist hold only 256. stencil_table[s, g * 256 + r] indexes E_g: values below 256 are live rows of partition g, 256 is the zero row, 257 + k * 64 + j is row j of the block from partition g - o_k, named only when that partition exists. Padding rows hold only 256; rows r below 160 name no block. bounds holds lower, cutoff and upper in this order: lower between -9 and -5, cutoff between -1.5 and 1.5, upper between 21 and 26.
All inputs are finite; a program needn't handle non-finite values.
Results may differ from a plain program's by a relative error of at most 0.0018.
Values may be sent and summed in bfloat16 or wider, within the bound.
A program may use at most 64 MiB of HBM per device.

v0:
```python
import jax
import jax.numpy as jnp
from jax import lax
from jax.sharding import PartitionSpec as P

SPAN = 6
DEGREE = 3


DIFFERENCE_WEIGHTS = (
    -5369.0 / 1800.0,
    12.0 / 7.0,
    -15.0 / 56.0,
    10.0 / 189.0,
    -1.0 / 112.0,
    2.0 / 1925.0,
    -1.0 / 16632.0,
)
KINETIC_SCALE = 0.5 / 0.49
CENTRE_WEIGHT = -3.0 * KINETIC_SCALE * DIFFERENCE_WEIGHTS[0]


def passed_along(block, axis, distance):
    devices = range(lax.axis_size(axis))
    route = [(i - distance, i) for i in devices if i - distance in devices]
    return lax.ppermute(block, axis, route)


def apply_stencil(extended, local_table, fields, potentials):
    result = (potentials + CENTRE_WEIGHT)[:, None] * fields
    for neighbour in range(local_table.shape[0]):
        weight = -KINETIC_SCALE * DIFFERENCE_WEIGHTS[neighbour % SPAN + 1]
        result = result + weight * jnp.take(extended, local_table[neighbour], axis=0)
    return result


def boundary_blocks(own_rows, send_rows):
    half_slots = send_rows.shape[1] // 2
    received = []
    for slot_index in range(2 * half_slots):
        offset = slot_index - half_slots if slot_index < half_slots else slot_index - half_slots + 1
        outgoing = jnp.take(own_rows, send_rows[0, slot_index], axis=0)
        received.append(
            passed_along(outgoing.astype(jnp.bfloat16), "grid", offset).astype(outgoing.dtype)
        )
    return jnp.concatenate(received, axis=0)


def operate(fields, potential, send_rows, stencil_table):
    zero_row = jnp.zeros((1, fields.shape[1]), jnp.float32)
    own_rows = jnp.concatenate([fields, zero_row], axis=0)
    extended = jnp.concatenate([own_rows, boundary_blocks(own_rows, send_rows)], axis=0)
    image = apply_stencil(extended, stencil_table, fields, potential)
    return image


def on_device(states, potential, bounds, point_count, send_rows, stencil_table):
    row_count = states.shape[0]
    live_rows = lax.broadcasted_iota(jnp.int32, (row_count, 1), 0) < point_count[0]
    previous = jnp.where(live_rows, states, 0.0)
    lower_bound = bounds[0]
    cutoff = bounds[1]
    upper_bound = bounds[2]
    half_width = (upper_bound - cutoff) / 2.0
    middle = (upper_bound + cutoff) / 2.0
    sigma_now = half_width / (lower_bound - middle)
    twice_inverse = 2.0 / sigma_now
    applied = operate(previous, potential, send_rows, stencil_table)
    current = (applied - middle * previous) * (sigma_now / half_width)
    for degree_index in range(DEGREE - 1):
        sigma_next = 1.0 / (twice_inverse - sigma_now)
        applied = operate(current, potential, send_rows, stencil_table)
        following = (applied - middle * current) * (
            2.0 * sigma_next / half_width
        ) - sigma_now * sigma_next * previous
        previous = current
        current = following
        sigma_now = sigma_next
    rounded = current.astype(jnp.bfloat16)
    grid_count = lax.axis_size("grid")
    band_count = lax.axis_size("band")
    scaling = 1.0 / (grid_count * row_count)
    every_band = lax.all_gather(rounded, "band", axis=1, tiled=True)
    per_device = rounded.shape[1] // grid_count
    arranged = every_band.reshape(row_count, grid_count, band_count, per_device)
    chosen = lax.dynamic_index_in_dim(arranged, lax.axis_index("band"), 2, keepdims=False).reshape(
        row_count, grid_count * per_device
    )
    partial_sums = jnp.einsum("pi,pj->ij", chosen, every_band, preferred_element_type=jnp.float32)
    summed = lax.psum_scatter(partial_sums, "grid", scatter_dimension=0, tiled=True)
    return (current, summed * scaling)


def solution(mesh):
    placed = (P("grid", "band"), P("grid"), P(), P("grid"), P("grid", None, None), P(None, "grid"))
    return jax.shard_map(
        on_device,
        mesh=mesh,
        in_specs=placed,
        out_specs=(P("grid", "band"), P(("grid", "band"), None)),
        check_vma=False,
    )
```

profile of v0, /device:TPU:0, one launch (start us, length us, event | category | flops | bytes accessed | tf_op | source)
XLA Modules:
  0.0 300.3 jit_solution(2098862100066533419)
XLA Ops:
  15.1 3.0 %collective-permute-start.3 = (bf16[64,128]{1,0:T(8,128)(2,1)S(1)}, bf16[64,128]{1,0:T(8,128)(2,1)S(1)}, u32[]{:S(2)}, u32[]{:S(2)}) collective-permute-start(bf16[64,128]{1,0:T(8,128)(2,1)S(1)} %select_convert_fusion.14), channel_id=1, source_target_pairs={{0,2},{2,4},{4,6},{6,8},{8,10},{10,12},{12,14},{14,16},{16,18},{18... | collective-permute-start | bytes 49160 | tf_op jit(solution)/shard_map/ppermute | solution.py:26
  18.8 5.5 %collective-permute-start.4 = (bf16[64,128]{1,0:T(8,128)(2,1)S(1)}, bf16[64,128]{1,0:T(8,128)(2,1)S(1)}, u32[]{:S(2)}, u32[]{:S(2)}) collective-permute-start(bf16[64,128]{1,0:T(8,128)(2,1)S(1)} %select_convert_fusion.13), channel_id=1, source_target_pairs={{0,4},{2,6},{4,8},{6,10},{8,12},{10,14},{12,16},{14,18},{16,20},{1... | collective-permute-start | bytes 49160 | tf_op jit(solution)/shard_map/ppermute | solution.py:26
  25.1 4.9 %collective-permute-start.5 = (bf16[64,128]{1,0:T(8,128)(2,1)S(1)}, bf16[64,128]{1,0:T(8,128)(2,1)S(1)}, u32[]{:S(2)}, u32[]{:S(2)}) collective-permute-start(bf16[64,128]{1,0:T(8,128)(2,1)S(1)} %select_convert_fusion.12), channel_id=1, source_target_pairs={{0,6},{2,8},{4,10},{6,12},{8,14},{10,16},{12,18},{14,20},{16,22},{... | collective-permute-start | bytes 49160 | tf_op jit(solution)/shard_map/ppermute | solution.py:26
  82.8 1.6 gather_fusion.41
  85.0 5.2 %fusion.80 = f32[256,128]{1,0:T(8,128)S(1)} fusion(f32[256,128]{1,0:T(8,128)} %gather_fusion.41, f32[256,128]{1,0:T(8,128)} %gather_fusion.40, f32[256,128]{1,0:T(8,128)S(1)} %gather_fusion.39, f32[256,128]{1,0:T(8,128)S(1)} %gather_fusion.38, f32[256,128]{1,0:T(8,128)S(1)} %gather_fusion.37, f32[256,128]{1,0:T(8,128)S(1)} %gather_fusion.36, ...), kind=kLoop, calls=%fused_computation.279 | loop fusion | flops 3702784 | bytes 4991240 | tf_op jit(solution)/shard_map/mul | solution.py:69
  95.1 4.6 %collective-permute-start.10 = (bf16[64,128]{1,0:T(8,128)(2,1)S(1)}, bf16[64,128]{1,0:T(8,128)(2,1)S(1)}, u32[]{:S(2)}, u32[]{:S(2)}) collective-permute-start(bf16[64,128]{1,0:T(8,128)(2,1)S(1)} %select_convert_fusion.7), channel_id=1, source_target_pairs={{0,4},{2,6},{4,8},{6,10},{8,12},{10,14},{12,16},{14,18},{16,20},{1... | collective-permute-start | bytes 49160 | tf_op jit(solution)/shard_map/ppermute | solution.py:26
  99.8 4.0 %collective-permute-start.11 = (bf16[64,128]{1,0:T(8,128)(2,1)S(1)}, bf16[64,128]{1,0:T(8,128)(2,1)S(1)}, u32[]{:S(2)}, u32[]{:S(2)}) collective-permute-start(bf16[64,128]{1,0:T(8,128)(2,1)S(1)} %select_convert_fusion.6), channel_id=1, source_target_pairs={{0,6},{2,8},{4,10},{6,12},{8,14},{10,16},{12,18},{14,20},{16,22},{... | collective-permute-start | bytes 49160 | tf_op jit(solution)/shard_map/ppermute | solution.py:26
  106.7 3.0 %collective-permute-start.9 = (bf16[64,128]{1,0:T(8,128)(2,1)S(1)}, bf16[64,128]{1,0:T(8,128)(2,1)S(1)}, u32[]{:S(2)}, u32[]{:S(2)}) collective-permute-start(bf16[64,128]{1,0:T(8,128)(2,1)S(1)} %select_convert_fusion.8), channel_id=1, source_target_pairs={{0,2},{2,4},{4,6},{6,8},{8,10},{10,12},{12,14},{14,16},{16,18},{18... | collective-permute-start | bytes 49160 | tf_op jit(solution)/shard_map/ppermute | solution.py:26
  111.5 5.3 %collective-permute-done.6 = bf16[64,128]{1,0:T(8,128)(2,1)S(1)} collective-permute-done((bf16[64,128]{1,0:T(8,128)(2,1)S(1)}, bf16[64,128]{1,0:T(8,128)(2,1)S(1)}, u32[]{:S(2)}, u32[]{:S(2)}) %collective-permute-start.6) | collective-permute-done | bytes 16416 | tf_op jit(solution)/shard_map/ppermute | solution.py:26
  134.6 1.5 gather_fusion.52
  150.8 1.5 gather_fusion.63
  153.7 1.5 gather_fusion.83
  155.2 5.3 %fusion.42 = f32[256,128]{1,0:T(8,128)S(1)} fusion(f32[256,128]{1,0:T(8,128)} %gather_fusion.83, f32[256,128]{1,0:T(8,128)} %gather_fusion.82, f32[256,128]{1,0:T(8,128)S(1)} %gather_fusion.81, f32[256,128]{1,0:T(8,128)S(1)} %gather_fusion.80, f32[256,128]{1,0:T(8,128)S(1)} %gather_fusion.79, f32[256,128]{1,0:T(8,128)S(1)} %gather_fusion.78, ...), kind=kLoop, calls=%fused_computation.205 | loop fusion | flops 3768320 | bytes 5122316 | tf_op jit(solution)/shard_map/sub | solution.py:73
  168.1 3.0 %collective-permute-start.15 = (bf16[64,128]{1,0:T(8,128)(2,1)S(1)}, bf16[64,128]{1,0:T(8,128)(2,1)S(1)}, u32[]{:S(2)}, u32[]{:S(2)}) collective-permute-start(bf16[64,128]{1,0:T(8,128)(2,1)S(1)} %select_convert_fusion.2), channel_id=1, source_target_pairs={{0,2},{2,4},{4,6},{6,8},{8,10},{10,12},{12,14},{14,16},{16,18},{18... | collective-permute-start | bytes 49160 | tf_op jit(solution)/shard_map/ppermute | solution.py:26
  171.2 4.6 %collective-permute-start.16 = (bf16[64,128]{1,0:T(8,128)(2,1)S(1)}, bf16[64,128]{1,0:T(8,128)(2,1)S(1)}, u32[]{:S(2)}, u32[]{:S(2)}) collective-permute-start(bf16[64,128]{1,0:T(8,128)(2,1)S(1)} %select_convert_fusion.1), channel_id=1, source_target_pairs={{0,4},{2,6},{4,8},{6,10},{8,12},{10,14},{12,16},{14,18},{16,20},{1... | collective-permute-start | bytes 49160 | tf_op jit(solution)/shard_map/ppermute | solution.py:26
  175.9 5.2 %collective-permute-start.17 = (bf16[64,128]{1,0:T(8,128)(2,1)S(1)}, bf16[64,128]{1,0:T(8,128)(2,1)S(1)}, u32[]{:S(2)}, u32[]{:S(2)}) collective-permute-start(bf16[64,128]{1,0:T(8,128)(2,1)S(1)} %select_convert_fusion), channel_id=1, source_target_pairs={{0,6},{2,8},{4,10},{6,12},{8,14},{10,16},{12,18},{14,20},{16,22},{... | collective-permute-start | bytes 49160 | tf_op jit(solution)/shard_map/ppermute | solution.py:26
  181.2 1.5 collective-permute-start.12
  182.9 3.4 %collective-permute-done.12 = bf16[64,128]{1,0:T(8,128)(2,1)S(1)} collective-permute-done((bf16[64,128]{1,0:T(8,128)(2,1)S(1)}, bf16[64,128]{1,0:T(8,128)(2,1)S(1)}, u32[]{:S(2)}, u32[]{:S(2)}) %collective-permute-start.12) | collective-permute-done | bytes 16416 | tf_op jit(solution)/shard_map/ppermute | solution.py:26
  205.4 1.5 gather_fusion.95
  221.6 1.5 gather_fusion.124
  223.3 1.5 gather_fusion.125
  224.9 6.2 %fusion.120 = (bf16[256,128]{1,0:T(8,128)(2,1)S(1)}, f32[256,128]{1,0:T(8,128)}) fusion(f32[256,128]{1,0:T(8,128)S(1)} %fusion.80, f32[]{:T(128)S(6)} %mul.533, f32[]{:T(128)S(6)} %div.41, f32[256,128]{1,0:T(8,128)S(1)} %fusion.42, f32[]{:T(128)} %bitcast.43, f32[256,128]{1,0:T(8,128)} %gather_fusion.125, pred[256]{0:T(512)(128)(4,1)} %get-tuple-element.67, ...), kind=kLoop, calls=%fused_computation.502 | loop fusion | flops 3768320 | bytes 5187596 | tf_op jit(solution)/shard_map/convert_element_type | solution.py:79
  231.1 5.0 %all_gather.3 = bf16[256,256]{1,0:T(8,128)(2,1)S(1)} all-gather(bf16[256,128]{1,0:T(8,128)(2,1)S(1)} %get-tuple-element.4), channel_id=1, replica_groups=mesh['grid'=16,'band'=2] {'band'}, dimensions={1}, use_global_device_ids=true | all-gather | bytes 196608 | tf_op jit(solution)/shard_map/all_gather | solution.py:83
  237.0 55.2 %reduce-scatter.2.cloned.1.call-done = f32[8,256]{1,0:T(8,128)} async-done(((f32[128,256]{1,0:T(8,128)}), f32[8,256]{1,0:T(8,128)}) %reduce-scatter.2.cloned.1.call-update) | async-done | bytes 8208 | tf_op jit(solution)/shard_map/reduce_scatter | solution.py:90
  (416 shorter events, 145.2 us)
Async XLA Ops:
  7.2 285.0 %reduce-scatter.2.cloned.1.call-start = ((), (), s32[]{:S(2)}) async-start(), calls=%async_computation.1 | async-start | bytes 139264 | tf_op jit(solution)/shard_map/reduce_scatter | solution.py:90
  8.0 35.0 %copy-start.19 = (pred[64]{0:T(512)(128)(4,1)}, pred[64]{0:T(512)(128)(4,1)S(1)}, u32[]{:S(2)}) copy-start(pred[64]{0:T(512)(128)(4,1)S(1)} %get-tuple-element.60) | copy-start | bytes 196
  11.0 32.1 %collective-permute-start.1 = (bf16[64,128]{1,0:T(8,128)(2,1)S(1)}, bf16[64,128]{1,0:T(8,128)(2,1)S(1)}, u32[]{:S(2)}, u32[]{:S(2)}) collective-permute-start(bf16[64,128]{1,0:T(8,128)(2,1)S(1)} %select_convert_fusion.16), channel_id=1, source_target_pairs={{4,0},{6,2},{8,4},{10,6},{12,8},{14,10},{16,12},{18,14},{20,16},{2... | collective-permute-start | bytes 49160 | tf_op jit(solution)/shard_map/ppermute | solution.py:26
  13.0 35.1 %collective-permute-start.2 = (bf16[64,128]{1,0:T(8,128)(2,1)S(1)}, bf16[64,128]{1,0:T(8,128)(2,1)S(1)}, u32[]{:S(2)}, u32[]{:S(2)}) collective-permute-start(bf16[64,128]{1,0:T(8,128)(2,1)S(1)} %select_convert_fusion.15), channel_id=1, source_target_pairs={{2,0},{4,2},{6,4},{8,6},{10,8},{12,10},{14,12},{16,14},{18,16},{20... | collective-permute-start | bytes 49160 | tf_op jit(solution)/shard_map/ppermute | solution.py:26
  15.1 33.0 %collective-permute-start.3 = (bf16[64,128]{1,0:T(8,128)(2,1)S(1)}, bf16[64,128]{1,0:T(8,128)(2,1)S(1)}, u32[]{:S(2)}, u32[]{:S(2)}) collective-permute-start(bf16[64,128]{1,0:T(8,128)(2,1)S(1)} %select_convert_fusion.14), channel_id=1, source_target_pairs={{0,2},{2,4},{4,6},{6,8},{8,10},{10,12},{12,14},{14,16},{16,18},{18... | collective-permute-start | bytes 49160 | tf_op jit(solution)/shard_map/ppermute | solution.py:26
  18.8 29.3 %collective-permute-start.4 = (bf16[64,128]{1,0:T(8,128)(2,1)S(1)}, bf16[64,128]{1,0:T(8,128)(2,1)S(1)}, u32[]{:S(2)}, u32[]{:S(2)}) collective-permute-start(bf16[64,128]{1,0:T(8,128)(2,1)S(1)} %select_convert_fusion.13), channel_id=1, source_target_pairs={{0,4},{2,6},{4,8},{6,10},{8,12},{10,14},{12,16},{14,18},{16,20},{1... | collective-permute-start | bytes 49160 | tf_op jit(solution)/shard_map/ppermute | solution.py:26
  25.1 23.0 %collective-permute-start.5 = (bf16[64,128]{1,0:T(8,128)(2,1)S(1)}, bf16[64,128]{1,0:T(8,128)(2,1)S(1)}, u32[]{:S(2)}, u32[]{:S(2)}) collective-permute-start(bf16[64,128]{1,0:T(8,128)(2,1)S(1)} %select_convert_fusion.12), channel_id=1, source_target_pairs={{0,6},{2,8},{4,10},{6,12},{8,14},{10,16},{12,18},{14,20},{16,22},{... | collective-permute-start | bytes 49160 | tf_op jit(solution)/shard_map/ppermute | solution.py:26
  41.7 35.7 %copy-start.15 = (s32[1024]{0:T(1024)}, s32[1024]{0:T(1024)S(1)}, u32[]{:S(2)}) copy-start(s32[1024]{0:T(1024)S(1)} %pad_clamp_fusion.22) | copy-start | bytes 12292
  41.7 37.0 %copy-start.16 = (s32[1024]{0:T(1024)}, s32[1024]{0:T(1024)S(1)}, u32[]{:S(2)}) copy-start(s32[1024]{0:T(1024)S(1)} %pad_clamp_fusion.21) | copy-start | bytes 12292
  42.3 37.8 %copy-start.17 = (s32[1024]{0:T(1024)}, s32[1024]{0:T(1024)S(1)}, u32[]{:S(2)}) copy-start(s32[1024]{0:T(1024)S(1)} %pad_clamp_fusion.20) | copy-start | bytes 12292
  43.1 38.4 %copy-start.18 = (s32[1024]{0:T(1024)}, s32[1024]{0:T(1024)S(1)}, u32[]{:S(2)}) copy-start(s32[1024]{0:T(1024)S(1)} %pad_clamp_fusion.1) | copy-start | bytes 12292
  43.1 5.1 %collective-permute-start = (bf16[64,128]{1,0:T(8,128)(2,1)S(1)}, bf16[64,128]{1,0:T(8,128)(2,1)S(1)}, u32[]{:S(2)}, u32[]{:S(2)}) collective-permute-start(bf16[64,128]{1,0:T(8,128)(2,1)S(1)} %select_convert_fusion.17), channel_id=1, source_target_pairs={{6,0},{8,2},{10,4},{12,6},{14,8},{16,10},{18,12},{20,14},{22,16},{... | collective-permute-start | bytes 49160 | tf_op jit(solution)/shard_map/ppermute | solution.py:26
  95.1 14.8 %collective-permute-start.10 = (bf16[64,128]{1,0:T(8,128)(2,1)S(1)}, bf16[64,128]{1,0:T(8,128)(2,1)S(1)}, u32[]{:S(2)}, u32[]{:S(2)}) collective-permute-start(bf16[64,128]{1,0:T(8,128)(2,1)S(1)} %select_convert_fusion.7), channel_id=1, source_target_pairs={{0,4},{2,6},{4,8},{6,10},{8,12},{10,14},{12,16},{14,18},{16,20},{1... | collective-permute-start | bytes 49160 | tf_op jit(solution)/shard_map/ppermute | solution.py:26
  99.8 11.7 %collective-permute-start.11 = (bf16[64,128]{1,0:T(8,128)(2,1)S(1)}, bf16[64,128]{1,0:T(8,128)(2,1)S(1)}, u32[]{:S(2)}, u32[]{:S(2)}) collective-permute-start(bf16[64,128]{1,0:T(8,128)(2,1)S(1)} %select_convert_fusion.6), channel_id=1, source_target_pairs={{0,6},{2,8},{4,10},{6,12},{8,14},{10,16},{12,18},{14,20},{16,22},{... | collective-permute-start | bytes 49160 | tf_op jit(solution)/shard_map/ppermute | solution.py:26
  103.9 7.6 %collective-permute-start.7 = (bf16[64,128]{1,0:T(8,128)(2,1)S(1)}, bf16[64,128]{1,0:T(8,128)(2,1)S(1)}, u32[]{:S(2)}, u32[]{:S(2)}) collective-permute-start(bf16[64,128]{1,0:T(8,128)(2,1)S(1)} %select_convert_fusion.10), channel_id=1, source_target_pairs={{4,0},{6,2},{8,4},{10,6},{12,8},{14,10},{16,12},{18,14},{20,16},{2... | collective-permute-start | bytes 49160 | tf_op jit(solution)/shard_map/ppermute | solution.py:26
  105.3 6.2 %collective-permute-start.8 = (bf16[64,128]{1,0:T(8,128)(2,1)S(1)}, bf16[64,128]{1,0:T(8,128)(2,1)S(1)}, u32[]{:S(2)}, u32[]{:S(2)}) collective-permute-start(bf16[64,128]{1,0:T(8,128)(2,1)S(1)} %select_convert_fusion.9), channel_id=1, source_target_pairs={{2,0},{4,2},{6,4},{8,6},{10,8},{12,10},{14,12},{16,14},{18,16},{20... | collective-permute-start | bytes 49160 | tf_op jit(solution)/shard_map/ppermute | solution.py:26
  106.7 4.8 %collective-permute-start.9 = (bf16[64,128]{1,0:T(8,128)(2,1)S(1)}, bf16[64,128]{1,0:T(8,128)(2,1)S(1)}, u32[]{:S(2)}, u32[]{:S(2)}) collective-permute-start(bf16[64,128]{1,0:T(8,128)(2,1)S(1)} %select_convert_fusion.8), channel_id=1, source_target_pairs={{0,2},{2,4},{4,6},{6,8},{8,10},{10,12},{12,14},{14,16},{16,18},{18... | collective-permute-start | bytes 49160 | tf_op jit(solution)/shard_map/ppermute | solution.py:26
  109.8 7.0 %collective-permute-start.6 = (bf16[64,128]{1,0:T(8,128)(2,1)S(1)}, bf16[64,128]{1,0:T(8,128)(2,1)S(1)}, u32[]{:S(2)}, u32[]{:S(2)}) collective-permute-start(bf16[64,128]{1,0:T(8,128)(2,1)S(1)} %select_convert_fusion.11), channel_id=1, source_target_pairs={{6,0},{8,2},{10,4},{12,6},{14,8},{16,10},{18,12},{20,14},{22,16},{... | collective-permute-start | bytes 49160 | tf_op jit(solution)/shard_map/ppermute | solution.py:26
  165.3 15.9 %collective-permute-start.13 = (bf16[64,128]{1,0:T(8,128)(2,1)S(1)}, bf16[64,128]{1,0:T(8,128)(2,1)S(1)}, u32[]{:S(2)}, u32[]{:S(2)}) collective-permute-start(bf16[64,128]{1,0:T(8,128)(2,1)S(1)} %select_convert_fusion.4), channel_id=1, source_target_pairs={{4,0},{6,2},{8,4},{10,6},{12,8},{14,10},{16,12},{18,14},{20,16},{2... | collective-permute-start | bytes 49160 | tf_op jit(solution)/shard_map/ppermute | solution.py:26
  166.7 16.1 %collective-permute-start.14 = (bf16[64,128]{1,0:T(8,128)(2,1)S(1)}, bf16[64,128]{1,0:T(8,128)(2,1)S(1)}, u32[]{:S(2)}, u32[]{:S(2)}) collective-permute-start(bf16[64,128]{1,0:T(8,128)(2,1)S(1)} %select_convert_fusion.3), channel_id=1, source_target_pairs={{2,0},{4,2},{6,4},{8,6},{10,8},{12,10},{14,12},{16,14},{18,16},{20... | collective-permute-start | bytes 49160 | tf_op jit(solution)/shard_map/ppermute | solution.py:26
  168.1 14.7 %collective-permute-start.15 = (bf16[64,128]{1,0:T(8,128)(2,1)S(1)}, bf16[64,128]{1,0:T(8,128)(2,1)S(1)}, u32[]{:S(2)}, u32[]{:S(2)}) collective-permute-start(bf16[64,128]{1,0:T(8,128)(2,1)S(1)} %select_convert_fusion.2), channel_id=1, source_target_pairs={{0,2},{2,4},{4,6},{6,8},{8,10},{10,12},{12,14},{14,16},{16,18},{18... | collective-permute-start | bytes 49160 | tf_op jit(solution)/shard_map/ppermute | solution.py:26
  171.2 11.6 %collective-permute-start.16 = (bf16[64,128]{1,0:T(8,128)(2,1)S(1)}, bf16[64,128]{1,0:T(8,128)(2,1)S(1)}, u32[]{:S(2)}, u32[]{:S(2)}) collective-permute-start(bf16[64,128]{1,0:T(8,128)(2,1)S(1)} %select_convert_fusion.1), channel_id=1, source_target_pairs={{0,4},{2,6},{4,8},{6,10},{8,12},{10,14},{12,16},{14,18},{16,20},{1... | collective-permute-start | bytes 49160 | tf_op jit(solution)/shard_map/ppermute | solution.py:26
  175.9 7.0 %collective-permute-start.17 = (bf16[64,128]{1,0:T(8,128)(2,1)S(1)}, bf16[64,128]{1,0:T(8,128)(2,1)S(1)}, u32[]{:S(2)}, u32[]{:S(2)}) collective-permute-start(bf16[64,128]{1,0:T(8,128)(2,1)S(1)} %select_convert_fusion), channel_id=1, source_target_pairs={{0,6},{2,8},{4,10},{6,12},{8,14},{10,16},{12,18},{14,20},{16,22},{... | collective-permute-start | bytes 49160 | tf_op jit(solution)/shard_map/ppermute | solution.py:26
  181.2 5.1 %collective-permute-start.12 = (bf16[64,128]{1,0:T(8,128)(2,1)S(1)}, bf16[64,128]{1,0:T(8,128)(2,1)S(1)}, u32[]{:S(2)}, u32[]{:S(2)}) collective-permute-start(bf16[64,128]{1,0:T(8,128)(2,1)S(1)} %select_convert_fusion.5), channel_id=1, source_target_pairs={{6,0},{8,2},{10,4},{12,6},{14,8},{16,10},{18,12},{20,14},{22,16},{... | collective-permute-start | bytes 49160 | tf_op jit(solution)/shard_map/ppermute | solution.py:26
  (65 other events, 503.5 us)
Sparse Core Ops, SparseCore 0:
  237.1 55.0 reduce-scatter.1
where the time goes:
time: 303 us; the launch traced here: 300 us
  local copies, waits for them, and re-layouts  129 us (43%)
  waiting for transfers between devices  64 us (21%)
  starting transfers between devices  50 us (17%)
  other arithmetic  32.3 us (11%)
  between operations  19.6 us (6%)
  blocking collectives  4.96 us (2%)
    gather x108, local copies, waits for them, and re-layouts, apply_stencil(): jnp.take(extended, local_table[neighbour], axis=0)  110 us
    reduce_scatter x1, waiting for transfers between devices, on_device(): lax.psum_scatter(partial_sums, 'grid', scatter_dimension=0, tiled=True)  55.2 us
    ppermute x18, starting transfers between devices, passed_along(): return lax.ppermute(block, axis, route)  50 us
    gather x18, local copies, waits for them, and re-layouts, boundary_blocks(): outgoing = jnp.take(own_rows, send_rows[0, slot_index], axis=0)  13.2 us
    and x18, other arithmetic, apply_stencil(): jnp.take(extended, local_table[neighbour], axis=0)  10.2 us
    ppermute x18, waiting for transfers between devices, passed_along(): return lax.ppermute(block, axis, route)  8.78 us
    convert_element_type x1, other arithmetic, on_device(): rounded = current.astype(jnp.bfloat16)  6.18 us
  transfers between devices with their start and end apart: 19, of which 3 were waited for; matrix products, arithmetic and copies ran while one was open for 5% of the time, Pallas kernels for 0%

commit v1 on v0

v1 whole, which is shorter than its diff:
```python
import functools

import jax
import jax.numpy as jnp
from jax import lax
from jax.experimental import pallas as pl
from jax.experimental.pallas import tpu as pltpu
from jax.sharding import PartitionSpec as P

SPAN = 6
DEGREE = 3
INNER = 160

DIFFERENCE_WEIGHTS = (
    -5369.0 / 1800.0,
    12.0 / 7.0,
    -15.0 / 56.0,
    10.0 / 189.0,
    -1.0 / 112.0,
    2.0 / 1925.0,
    -1.0 / 16632.0,
)
KINETIC_SCALE = 0.5 / 0.49
CENTRE_WEIGHT = -3.0 * KINETIC_SCALE * DIFFERENCE_WEIGHTS[0]

MESH = pl.DeviceIdType.MESH
F32 = jnp.float32
BF16 = jnp.bfloat16


def dot(a, b):
    return jnp.dot(a, b, preferred_element_type=F32)


def gram(x):
    return lax.dot_general(x, x, (((0,), (0,)), ((), ())), preferred_element_type=F32)


def halves(x):
    high = x.astype(BF16)
    return high, (x - high.astype(F32)).astype(BF16)


def offset_of(slot, reach):
    return slot - reach if slot < reach else slot - reach + 1


def kernel(
    n_grid, n_band, bounds, count, states, potential, send_rows, table, filtered, margin,
    table_pad, send_pad, picks, near_hi, near_lo, far_hi, far_lo, out_box, in_box, bands, total,
    share_out, share_in, halo_sent, halo_got, band_sent, band_got, share_sent, share_got,
):
    rows, width = states.shape
    slots, halo = send_rows.shape[1:]
    reach = slots // 2
    stencil = table.shape[0]
    outer = rows - INNER
    per = margin.shape[0]
    g = lax.axis_index("grid")
    b = lax.axis_index("band")

    in_box[...] = jnp.zeros_like(in_box)
    barrier = pltpu.get_barrier_semaphore()
    for d in range(1, n_grid):
        pl.semaphore_signal(barrier, inc=1, device_id={"grid": lax.rem(g + d, n_grid)}, device_id_type=MESH)
    for d in range(1, n_band):
        pl.semaphore_signal(barrier, inc=1, device_id={"band": lax.rem(b + d, n_band)}, device_id_type=MESH)

    send_pad[...] = jnp.full(send_pad.shape, -1.0, F32)
    send_pad[:slots, :halo] = send_rows[0].astype(F32)
    send_columns = send_pad[...].T
    lanes = lax.broadcasted_iota(jnp.int32, (halo, rows), 1).astype(F32)
    for k in range(slots):
        hit = send_columns[:halo, k : k + 1] == lanes
        picks[k * halo : (k + 1) * halo, :] = jnp.where(hit, 1.0, 0.0).astype(BF16)

    def halo_copy(i, k, target):
        return pltpu.make_async_remote_copy(
            src_ref=out_box.at[i, k],
            dst_ref=in_box.at[i, k],
            send_sem=halo_sent.at[i, k],
            recv_sem=halo_got.at[i, k],
            device_id={"grid": target},
            device_id_type=MESH,
        )

    def send_halo(i, field):
        out_box[i] = dot(picks[...], field.astype(BF16)).astype(BF16).reshape(slots, halo, width)
        if i == 0:
            pl.semaphore_wait(barrier, n_grid - 1 + n_band - 1)
        for k in range(slots):
            target = g + offset_of(k, reach)

            @pl.when(jnp.logical_and(target >= 0, target < n_grid))
            def _():
                halo_copy(i, k, target).start()

    def wait_halo(i):
        for k in range(slots):
            source = g - offset_of(k, reach)

            @pl.when(jnp.logical_and(source >= 0, source < n_grid))
            def _():
                halo_copy(i, k, g).wait_recv()

    live = lax.broadcasted_iota(jnp.int32, (rows, width), 0) < count[0]
    previous = jnp.zeros((rows, width), F32)
    current = jnp.where(live, states[...], 0.0)
    send_halo(0, current)

    table_pad[...] = jnp.zeros_like(table_pad)
    table_pad[:stencil, :] = table[...].astype(F32)
    table_pad[stencil : stencil + 1, :] = potential[...]
    columns = table_pad[...].T
    weights = [-KINETIC_SCALE * DIFFERENCE_WEIGHTS[s % SPAN + 1] for s in range(stencil)]

    def weigh(first, size, start, extent):
        ids = (lax.broadcasted_iota(jnp.int32, (size, extent), 1) + start).astype(F32)
        acc = jnp.zeros((size, extent), F32)
        for s in range(stencil):
            acc = acc + jnp.where(columns[first : first + size, s : s + 1] == ids, weights[s], 0.0)
        return halves(acc)

    chunk = 32
    for first in range(0, rows, chunk):
        near_hi[first : first + chunk, :], near_lo[first : first + chunk, :] = weigh(first, chunk, 0, rows)
    for first in range(INNER, rows, chunk):
        at = slice(first - INNER, first - INNER + chunk)
        far_hi[at, :], far_lo[at, :] = weigh(first, chunk, rows + 1, slots * halo)

    def spread(value):
        return jnp.full((8, width), value, F32)

    lower, cutoff, upper = spread(bounds[0]), spread(bounds[1]), spread(bounds[2])
    half_width = (upper - cutoff) / 2.0
    middle = (upper + cutoff) / 2.0
    sigma = half_width / (lower - middle)
    twice_inverse = 2.0 / sigma
    diagonal = columns[:, stencil : stencil + 1] + CENTRE_WEIGHT - middle[:1, :]

    def near(field):
        high, low = halves(field)
        a = near_hi[...]
        return diagonal * field + (dot(a, high) + (dot(a, low) + dot(near_lo[...], high)))

    def far(i):
        box = in_box[i].reshape(slots * halo, width)
        return dot(far_hi[...], box) + dot(far_lo[...], box)

    gain = sigma / half_width
    back = jnp.zeros_like(sigma)
    for i in range(DEGREE):
        own = near(current)
        base = own * gain[:1, :] - back[:1, :] * previous
        if i < DEGREE - 1:
            wait_halo(i)
            outer_rows = base[INNER:] + far(i) * gain[:1, :]
            previous, current = current, jnp.concatenate([base[:INNER], outer_rows], axis=0)
            send_halo(i + 1, current)
            sigma_next = 1.0 / (twice_inverse - sigma)
            gain = 2.0 * sigma_next / half_width
            back = sigma * sigma_next
            sigma = sigma_next

    def band_copy(part, d):
        at = pl.ds(0, INNER) if part == 0 else pl.ds(INNER, outer)
        place = bands.at[b, at]
        return pltpu.make_async_remote_copy(
            src_ref=place,
            dst_ref=place,
            send_sem=band_sent.at[part, d - 1],
            recv_sem=band_got.at[part, d - 1],
            device_id={"band": lax.rem(b + d, n_band)},
            device_id_type=MESH,
        )

    def every_band(at):
        return jnp.concatenate([bands[j, at, :] for j in range(n_band)], axis=1)

    top, bottom = slice(0, INNER), slice(INNER, rows)
    filtered[top, :] = base[top]
    bands[b, top, :] = base[top].astype(BF16)
    for d in range(1, n_band):
        band_copy(0, d).start()
    for d in range(1, n_band):
        band_copy(0, d).wait_recv()
    total[...] = gram(every_band(top))
    wait_halo(DEGREE - 1)
    last = base[bottom] + far(DEGREE - 1) * gain[:1, :]
    bands[b, bottom, :] = last.astype(BF16)
    for d in range(1, n_band):
        band_copy(1, d).start()
    filtered[bottom, :] = last
    for d in range(1, n_band):
        band_copy(1, d).wait_recv()
    total[...] += gram(every_band(bottom))

    def share_copy(d):
        return pltpu.make_async_remote_copy(
            src_ref=share_out.at[d - 1],
            dst_ref=share_in.at[d - 1],
            send_sem=share_sent.at[d - 1],
            recv_sem=share_got.at[d - 1],
            device_id={"grid": lax.rem(g + d, n_grid)},
            device_id_type=MESH,
        )

    def share_of(owner):
        if per % 8 == 0:
            return total[pl.ds(pl.multiple_of((owner * n_band + b) * per, per), per), :]
        group = total[pl.ds(pl.multiple_of(owner * n_band * per, n_band * per), n_band * per), :]
        chosen = group[:per]
        for j in range(1, n_band):
            chosen = jnp.where(b == j, group[j * per : (j + 1) * per], chosen)
        return chosen

    for d in range(1, n_grid):
        share_out[d - 1] = share_of(lax.rem(g + d, n_grid)).astype(BF16)
    for d in range(1, n_grid):
        share_copy(d).start()
    result = share_of(g)
    for d in range(1, n_grid):
        share_copy(d).wait_recv()
    for d in range(1, n_grid):
        result = result + share_in[d - 1].astype(F32)
    margin[...] = result * (1.0 / (n_grid * rows))

    for i in range(DEGREE):
        for k in range(slots):
            target = g + offset_of(k, reach)

            @pl.when(jnp.logical_and(target >= 0, target < n_grid))
            def _():
                halo_copy(i, k, target).wait_send()

    for d in range(1, n_band):
        band_copy(0, d).wait_send()
        band_copy(1, d).wait_send()
    for d in range(1, n_grid):
        share_copy(d).wait_send()


def on_device(n_grid, n_band, states, potential, bounds, point_count, send_rows, stencil_table):
    rows, width = states.shape
    slots, halo = send_rows.shape[1:]
    total_bands = width * n_band
    per = total_bands // (n_grid * n_band)
    vmem = pl.BlockSpec(memory_space=pltpu.VMEM)
    smem = pl.BlockSpec(memory_space=pltpu.SMEM)
    dma = pltpu.SemaphoreType.DMA
    return pl.pallas_call(
        functools.partial(kernel, n_grid, n_band),
        out_shape=(
            jax.ShapeDtypeStruct((rows, width), F32),
            jax.ShapeDtypeStruct((per, total_bands), F32),
        ),
        in_specs=[smem, smem, vmem, vmem, vmem, vmem],
        out_specs=(vmem, vmem),
        scratch_shapes=[
            pltpu.VMEM((128, rows), F32),
            pltpu.VMEM((128, 128), F32),
            pltpu.VMEM((slots * halo, rows), BF16),
            pltpu.VMEM((rows, rows), BF16),
            pltpu.VMEM((rows, rows), BF16),
            pltpu.VMEM((rows - INNER, slots * halo), BF16),
            pltpu.VMEM((rows - INNER, slots * halo), BF16),
            pltpu.VMEM((DEGREE, slots, halo, width), BF16),
            pltpu.VMEM((DEGREE, slots, halo, width), BF16),
            pltpu.VMEM((n_band, rows, width), BF16),
            pltpu.VMEM((total_bands, total_bands), F32),
            pltpu.VMEM((n_grid - 1, per, total_bands), BF16),
            pltpu.VMEM((n_grid - 1, per, total_bands), BF16),
            dma((DEGREE, slots)),
            dma((DEGREE, slots)),
            dma((2, n_band - 1)),
            dma((2, n_band - 1)),
            dma((n_grid - 1,)),
            dma((n_grid - 1,)),
        ],
        compiler_params=pltpu.CompilerParams(collective_id=0, has_side_effects=True),
    )(bounds, point_count, states, potential.reshape(1, rows), send_rows, stencil_table)


def solution(mesh):
    placed = (P("grid", "band"), P("grid"), P(), P("grid"), P("grid", None, None), P(None, "grid"))
    return jax.shard_map(
        functools.partial(on_device, mesh.shape["grid"], mesh.shape["band"]),
        mesh=mesh,
        in_specs=placed,
        out_specs=(P("grid", "band"), P(("grid", "band"), None)),
        check_vma=False,
    )
```

time: 303 us -> 30.1 us (0.10)
  local copies, waits for them, and re-layouts: 129 us -> 2.79 us
  waiting for transfers between devices: 64 us -> 0 us
  starting transfers between devices: 50 us -> 0 us
  other arithmetic: 32.3 us -> 0 us
  Pallas kernels: 0 us -> 25.8 us
  between operations: 19.6 us -> 1.31 us
  blocking collectives: 4.96 us -> 0 us
    gather x126 -> x0, local copies, waits for them, and re-layouts: 123 us -> none  [the longest x108 110 us: apply_stencil(): jnp.take(extended, local_table[neighbour], axis=0)]
    reduce_scatter x1 -> x0, waiting for transfers between devices: 55.2 us -> none  [on_device(): lax.psum_scatter(partial_sums, 'grid', scatter_dimension=0, tiled=True)]
    ppermute x18 -> x0, starting transfers between devices: 50 us -> none  [passed_along(): return lax.ppermute(block, axis, route)]
    pallas_call x0 -> x1, Pallas kernels: none -> 25.8 us  [on_device(): pl.pallas_call(functools.partial(kernel, n_grid, n_band), out_shape=(jax....]
    and x19 -> x0, other arithmetic: 11 us -> none  [the longest x18 10.2 us: apply_stencil(): jnp.take(extended, local_table[neighbour], axis=0)]
    ppermute x18 -> x0, waiting for transfers between devices: 8.78 us -> none  [passed_along(): return lax.ppermute(block, axis, route)]
    convert_element_type x19 -> x0, other arithmetic: 7.54 us -> none  [the longest x1 6.18 us: on_device(): rounded = current.astype(jnp.bfloat16)]
    mul x2 -> x0, other arithmetic: 6.53 us -> none  [the longest x1 5.23 us: on_device(): current = (applied - middle * previous) * (sigma_now / half_width)]
  transfers between devices with their start and end apart: 19 -> 0, of which waited for: 3 -> 0; matrix products, arithmetic and copies ran while one was open for 5% -> 0% of each run, Pallas kernels for 0% -> 0%
where the time goes in v1:
time: 30.1 us; the launch traced here: 29.9 us
  Pallas kernels  25.8 us (86%)
  local copies, waits for them, and re-layouts  2.79 us (9%)
  between operations  1.31 us (4%)
    pallas_call x1, Pallas kernels, on_device(): pl.pallas_call(functools.partial(kernel, n_grid, n_band), out_shape=(jax....  25.8 us
    unnamed x7, local copies, waits for them, and re-layouts  2.79 us

profile of v1, /device:TPU:0, one launch (start us, length us, event | category | flops | bytes accessed | tf_op | source)
XLA Modules:
  0.0 29.9 jit_solution(14292245660529412283)
XLA Ops:
  0.6 0.0 copy-start.1
  1.3 0.0 copy-done.1
  1.3 0.6 %copy.8.send_rows = s32[1,6,64]{2,1,0:T(8,128)} copy(s32[1,6,64]{2,0,1:T(1,128)S(1)} %copy-done.1) | data formatting | bytes 3072 | tf_op args[4]
  1.9 25.8 %shard_map.77 = (f32[256,128]{1,0:T(8,128)}, f32[8,256]{1,0:T(8,128)}) custom-call(f32[3]{0:T(128)} %bounds.1, s32[1]{0:T(128)S(6)} %copy.11.count, f32[256,128]{1,0:T(8,128)} %states.1, f32[1,256]{1,0:T(1,128)} %bitcast.1, s32[1,6,64]{2,1,0:T(8,128)} %copy.8.send_rows, s32[36,256]{1,0:T(8,128)} %table.1), custom_call_target="tpu_custom_call" | custom-call | tf_op jit(solution)/shard_map/pallas_call | solution.py:251
  27.7 0.0 copy-start
  27.8 1.6 %copy.12 = f32[256,128]{1,0:T(8,128)} copy(f32[256,128]{1,0:T(8,128)} %get-tuple-element.4) | data formatting | bytes 262144
  29.3 0.0 copy-done
  29.3 0.6 %copy.13 = f32[8,256]{1,0:T(8,128)} copy(f32[8,256]{1,0:T(8,128)S(1)} %copy-done) | data formatting | bytes 16384
Async XLA Ops:
  0.6 0.7 %copy-start.1 = (s32[1,6,64]{2,0,1:T(1,128)S(1)}, s32[1,6,64]{2,0,1:T(1,128)}, u32[]{:S(2)}) copy-start(s32[1,6,64]{2,0,1:T(1,128)} %param.10) | copy-start | bytes 4612
  27.7 1.6 %copy-start = (f32[8,256]{1,0:T(8,128)S(1)}, f32[8,256]{1,0:T(8,128)}, u32[]{:S(2)}) copy-start(f32[8,256]{1,0:T(8,128)} %get-tuple-element.5) | copy-start | bytes 24580

commit v2 on v1

--- a/solution.py
+++ b/solution.py
@@ -26,6 +26,7 @@
 MESH = pl.DeviceIdType.MESH
 F32 = jnp.float32
 BF16 = jnp.bfloat16
+VMEM_BYTES = 67043328
 
 
 def dot(a, b):
@@ -46,12 +47,12 @@
 
 
 def kernel(
-    n_grid, n_band, bounds, count, states, potential, send_rows, table, filtered, margin,
-    table_pad, send_pad, picks, near_hi, near_lo, far_hi, far_lo, out_box, in_box, bands, total,
+    n_grid, n_band, bounds_hbm, count_hbm, states_hbm, potential_hbm, send_rows_hbm, table_hbm, filtered, margin,
+    bounds, count, states, potential, send_rows, table, fetched, table_pad, send_pad, picks, near_hi, near_lo, far_hi, far_lo, out_box, in_box, bands, total,
     share_out, share_in, halo_sent, halo_got, band_sent, band_got, share_sent, share_got,
 ):
     rows, width = states.shape
-    slots, halo = send_rows.shape[1:]
+    slots, _, halo = send_rows.shape
     reach = slots // 2
     stencil = table.shape[0]
     outer = rows - INNER
@@ -59,6 +60,21 @@
     g = lax.axis_index("grid")
     b = lax.axis_index("band")
 
+    fetches = [
+        pltpu.make_async_copy(source, place, fetched.at[i])
+        for i, (source, place) in enumerate(
+            (
+                (send_rows_hbm, send_rows),
+                (count_hbm, count),
+                (states_hbm, states),
+                (table_hbm, table),
+                (potential_hbm, potential),
+                (bounds_hbm, bounds),
+            )
+        )
+    ]
+    for fetch in fetches:
+        fetch.start()
     in_box[...] = jnp.zeros_like(in_box)
     barrier = pltpu.get_barrier_semaphore()
     for d in range(1, n_grid):
@@ -67,7 +83,9 @@
         pl.semaphore_signal(barrier, inc=1, device_id={"band": lax.rem(b + d, n_band)}, device_id_type=MESH)
 
     send_pad[...] = jnp.full(send_pad.shape, -1.0, F32)
-    send_pad[:slots, :halo] = send_rows[0].astype(F32)
+    fetches[0].wait()
+    for k in range(slots):
+        send_pad[k : k + 1, :halo] = send_rows[k].astype(F32)
     send_columns = send_pad[...].T
     lanes = lax.broadcasted_iota(jnp.int32, (halo, rows), 1).astype(F32)
     for k in range(slots):
@@ -103,11 +121,15 @@
             def _():
                 halo_copy(i, k, g).wait_recv()
 
-    live = lax.broadcasted_iota(jnp.int32, (rows, width), 0) < count[0]
+    fetches[1].wait()
+    fetches[2].wait()
+    live = lax.broadcasted_iota(jnp.int32, (rows, width), 0) < count[...]
     previous = jnp.zeros((rows, width), F32)
     current = jnp.where(live, states[...], 0.0)
     send_halo(0, current)
 
+    fetches[3].wait()
+    fetches[4].wait()
     table_pad[...] = jnp.zeros_like(table_pad)
     table_pad[:stencil, :] = table[...].astype(F32)
     table_pad[stencil : stencil + 1, :] = potential[...]
@@ -128,10 +150,8 @@
         at = slice(first - INNER, first - INNER + chunk)
         far_hi[at, :], far_lo[at, :] = weigh(first, chunk, rows + 1, slots * halo)
 
-    def spread(value):
-        return jnp.full((8, width), value, F32)
-
-    lower, cutoff, upper = spread(bounds[0]), spread(bounds[1]), spread(bounds[2])
+    fetches[5].wait()
+    lower, cutoff, upper = (jnp.broadcast_to(bounds[:, j : j + 1], (8, width)) for j in range(3))
     half_width = (upper - cutoff) / 2.0
     middle = (upper + cutoff) / 2.0
     sigma = half_width / (lower - middle)
@@ -182,15 +202,15 @@
     bands[b, top, :] = base[top].astype(BF16)
     for d in range(1, n_band):
         band_copy(0, d).start()
-    for d in range(1, n_band):
-        band_copy(0, d).wait_recv()
-    total[...] = gram(every_band(top))
     wait_halo(DEGREE - 1)
     last = base[bottom] + far(DEGREE - 1) * gain[:1, :]
     bands[b, bottom, :] = last.astype(BF16)
     for d in range(1, n_band):
         band_copy(1, d).start()
     filtered[bottom, :] = last
+    for d in range(1, n_band):
+        band_copy(0, d).wait_recv()
+    total[...] = gram(every_band(top))
     for d in range(1, n_band):
         band_copy(1, d).wait_recv()
     total[...] += gram(every_band(bottom))
@@ -240,23 +260,43 @@
         share_copy(d).wait_send()
 
 
+def finish(filtered, margin, filtered_out, margin_out, sems):
+    copies = [
+        pltpu.make_async_copy(filtered, filtered_out, sems.at[0]),
+        pltpu.make_async_copy(margin, margin_out, sems.at[1]),
+    ]
+    for copy in copies:
+        copy.start()
+    for copy in copies:
+        copy.wait()
+
+
 def on_device(n_grid, n_band, states, potential, bounds, point_count, send_rows, stencil_table):
     rows, width = states.shape
     slots, halo = send_rows.shape[1:]
+    i32 = jnp.int32
     total_bands = width * n_band
     per = total_bands // (n_grid * n_band)
     vmem = pl.BlockSpec(memory_space=pltpu.VMEM)
-    smem = pl.BlockSpec(memory_space=pltpu.SMEM)
+    hbm = pl.BlockSpec(memory_space=pl.ANY)
     dma = pltpu.SemaphoreType.DMA
-    return pl.pallas_call(
+    outs = (
+        jax.ShapeDtypeStruct((rows, width), F32),
+        jax.ShapeDtypeStruct((per, total_bands), F32),
+    )
+    made = pl.pallas_call(
         functools.partial(kernel, n_grid, n_band),
-        out_shape=(
-            jax.ShapeDtypeStruct((rows, width), F32),
-            jax.ShapeDtypeStruct((per, total_bands), F32),
-        ),
-        in_specs=[smem, smem, vmem, vmem, vmem, vmem],
+        out_shape=tuple(pltpu.VMEM(out.shape, out.dtype) for out in outs),
+        in_specs=[pl.BlockSpec(memory_space=pltpu.HBM)] * 6,
         out_specs=(vmem, vmem),
         scratch_shapes=[
+            pltpu.VMEM((1, 3), F32),
+            pltpu.VMEM((1, 1), i32),
+            pltpu.VMEM((rows, width), F32),
+            pltpu.VMEM((1, rows), F32),
+            pltpu.VMEM((slots, 1, halo), i32),
+            pltpu.VMEM(stencil_table.shape, i32),
+            dma((6,)),
             pltpu.VMEM((128, rows), F32),
             pltpu.VMEM((128, 128), F32),
             pltpu.VMEM((slots * halo, rows), BF16),
@@ -277,8 +317,25 @@
             dma((n_grid - 1,)),
             dma((n_grid - 1,)),
         ],
-        compiler_params=pltpu.CompilerParams(collective_id=0, has_side_effects=True),
-    )(bounds, point_count, states, potential.reshape(1, rows), send_rows, stencil_table)
+        compiler_params=pltpu.CompilerParams(
+            collective_id=0, has_side_effects=True, vmem_limit_bytes=VMEM_BYTES - 8 * (rows * width + per * total_bands)
+        ),
+    )(
+        bounds.reshape(1, 3),
+        point_count.reshape(1, 1),
+        states,
+        potential.reshape(1, rows),
+        jnp.transpose(send_rows, (1, 0, 2)),
+        stencil_table,
+    )
+    return pl.pallas_call(
+        finish,
+        out_shape=outs,
+        in_specs=[vmem, vmem],
+        out_specs=(hbm, hbm),
+        scratch_shapes=[dma((2,))],
+        compiler_params=pltpu.CompilerParams(vmem_limit_bytes=24 * 1024 * 1024),
+    )(*made)
 
 
 def solution(mesh):

time: 30.1 us -> 26.4 us (0.88)
  local copies, waits for them, and re-layouts: 2.79 us -> 0 us
  Pallas kernels: 25.8 us -> 25 us
    unnamed x7 -> x0, local copies, waits for them, and re-layouts: 2.79 us -> none
    pallas_call x1 -> x2, Pallas kernels: 25.8 us -> 25 us  [the longest x1 24.3 us: on_device(): pl.pallas_call(functools.partial(kernel, n_grid, n_band), out_shape=tuple...]
where the time goes in v2:
time: 26.4 us; the launch traced here: 26.2 us
  Pallas kernels  25 us (95%)
  between operations  1.29 us (5%)
    pallas_call x1, Pallas kernels, on_device(): pl.pallas_call(functools.partial(kernel, n_grid, n_band), out_shape=tuple...  24.3 us
    pallas_call x1, Pallas kernels, on_device(): pl.pallas_call(finish, out_shape=outs, in_specs=[vmem, vmem], out_specs=(...  0.68 us

profile of v2, /device:TPU:0, one launch (start us, length us, event | category | flops | bytes accessed | tf_op | source)
XLA Modules:
  0.0 26.2 jit_solution(4013970192346821797)
XLA Ops:
  1.3 24.3 %shard_map.77 = (f32[256,128]{1,0:T(8,128)S(1)}, f32[8,256]{1,0:T(8,128)S(1)}) custom-call(f32[1,3]{1,0:T(1,128)} %bitcast.7, s32[1,1]{1,0:T(1,128)} %bitcast.4.count_hbm, f32[256,128]{1,0:T(8,128)} %states_hbm.1, f32[1,256]{1,0:T(1,128)} %bitcast.6, s32[6,1,64]{2,1,0:T(1,128)} %bitcast.5, s32[36,256]{1,0:T(8,128)} %table_hbm.1), custom_call_target="tpu_custom_call" | custom-call | tf_op jit(solution)/shard_map/pallas_call | solution.py:287
  25.6 0.7 %shard_map.78 = (f32[256,128]{1,0:T(8,128)}, f32[8,256]{1,0:T(8,128)}) custom-call(f32[256,128]{1,0:T(8,128)S(1)} %get-tuple-element.4.filtered, f32[8,256]{1,0:T(8,128)S(1)} %get-tuple-element.5.margin), custom_call_target="tpu_custom_call" | custom-call | tf_op jit(solution)/shard_map/pallas_call | solution.py:331

commit v3 on v2

--- a/solution.py
+++ b/solution.py
@@ -49,7 +49,7 @@
 def kernel(
     n_grid, n_band, bounds_hbm, count_hbm, states_hbm, potential_hbm, send_rows_hbm, table_hbm, filtered, margin,
     bounds, count, states, potential, send_rows, table, fetched, table_pad, send_pad, picks, near_hi, near_lo, far_hi, far_lo, out_box, in_box, bands, total,
-    share_out, share_in, halo_sent, halo_got, band_sent, band_got, share_sent, share_got,
+    share_out, share_in, greetings, passed_hi, passed_lo, halo_sent, halo_got, band_sent, band_got, share_sent, share_got,
 ):
     rows, width = states.shape
     slots, _, halo = send_rows.shape
@@ -59,6 +59,7 @@
     per = margin.shape[0]
     g = lax.axis_index("grid")
     b = lax.axis_index("band")
+    side = lax.rem(g // 2, 2)
 
     fetches = [
         pltpu.make_async_copy(source, place, fetched.at[i])
@@ -77,8 +78,33 @@
         fetch.start()
     in_box[...] = jnp.zeros_like(in_box)
     barrier = pltpu.get_barrier_semaphore()
-    for d in range(1, n_grid):
-        pl.semaphore_signal(barrier, inc=1, device_id={"grid": lax.rem(g + d, n_grid)}, device_id_type=MESH)
+    def at_distance(distance, act):
+        for target in (g - distance, g + distance):
+
+            @pl.when(jnp.logical_and(target >= 0, target < n_grid))
+            def _():
+                act(target)
+
+    def greet(semaphore, first, final):
+        for distance in range(first, final + 1):
+            at_distance(
+                distance,
+                lambda target: pl.semaphore_signal(
+                    semaphore, inc=1, device_id={"grid": target}, device_id_type=MESH
+                ),
+            )
+
+    def peers(first, final):
+        number = 0
+        for distance in range(first, final + 1):
+            for target in (g - distance, g + distance):
+                number = number + jnp.where(jnp.logical_and(target >= 0, target < n_grid), 1, 0)
+        return number
+
+    def greeted(semaphore, first, final):
+        pl.semaphore_wait(semaphore, peers(first, final))
+
+    greet(barrier, 1, min(reach, n_grid - 1))
     for d in range(1, n_band):
         pl.semaphore_signal(barrier, inc=1, device_id={"band": lax.rem(b + d, n_band)}, device_id_type=MESH)
 
@@ -102,12 +128,13 @@
             device_id_type=MESH,
         )
 
-    def send_halo(i, field):
-        out_box[i] = dot(picks[...], field.astype(BF16)).astype(BF16).reshape(slots, halo, width)
+    def send_halo(i, chosen):
+        out_box[i] = chosen.astype(BF16).reshape(slots, halo, width)
         if i == 0:
-            pl.semaphore_wait(barrier, n_grid - 1 + n_band - 1)
-        for k in range(slots):
-            target = g + offset_of(k, reach)
+            pl.semaphore_wait(barrier, n_band - 1 + peers(1, min(reach, n_grid - 1)))
+        for order in range(slots):
+            k = jnp.where(side == 0, order, slots - 1 - order)
+            target = g + k - reach + jnp.where(k < reach, 0, 1)
 
             @pl.when(jnp.logical_and(target >= 0, target < n_grid))
             def _():
@@ -126,7 +153,7 @@
     live = lax.broadcasted_iota(jnp.int32, (rows, width), 0) < count[...]
     previous = jnp.zeros((rows, width), F32)
     current = jnp.where(live, states[...], 0.0)
-    send_halo(0, current)
+    send_halo(0, dot(picks[...], current.astype(BF16)))
 
     fetches[3].wait()
     fetches[4].wait()
@@ -137,11 +164,20 @@
     weights = [-KINETIC_SCALE * DIFFERENCE_WEIGHTS[s % SPAN + 1] for s in range(stencil)]
 
     def weigh(first, size, start, extent):
-        ids = (lax.broadcasted_iota(jnp.int32, (size, extent), 1) + start).astype(F32)
-        acc = jnp.zeros((size, extent), F32)
-        for s in range(stencil):
-            acc = acc + jnp.where(columns[first : first + size, s : s + 1] == ids, weights[s], 0.0)
-        return halves(acc)
+        pieces = []
+        for begin in range(0, extent, 256):
+            wide = min(256, extent - begin)
+            ids = lax.broadcasted_iota(jnp.int32, (size, wide), 1).astype(F32).astype(BF16)
+            rows_of = (columns[first : first + size, :stencil] - float(start + begin)).astype(BF16)
+            one, none = jnp.ones((size, wide), BF16), jnp.zeros((size, wide), BF16)
+            acc = jnp.zeros((size, wide), F32)
+            for j in range(SPAN):
+                tally = none
+                for s in range(j, stencil, SPAN):
+                    tally = tally + jnp.where(rows_of[:, s : s + 1] == ids, one, none)
+                acc = acc + weights[j] * tally.astype(F32)
+            pieces.append(acc)
+        return halves(jnp.concatenate(pieces, axis=1))
 
     chunk = 32
     for first in range(0, rows, chunk):
@@ -149,6 +185,8 @@
     for first in range(INNER, rows, chunk):
         at = slice(first - INNER, first - INNER + chunk)
         far_hi[at, :], far_lo[at, :] = weigh(first, chunk, rows + 1, slots * halo)
+    passed_hi[...] = dot(picks[:, INNER:], far_hi[...]).astype(BF16)
+    passed_lo[...] = dot(picks[:, INNER:], far_lo[...]).astype(BF16)
 
     fetches[5].wait()
     lower, cutoff, upper = (jnp.broadcast_to(bounds[:, j : j + 1], (8, width)) for j in range(3))
@@ -173,10 +211,18 @@
         own = near(current)
         base = own * gain[:1, :] - back[:1, :] * previous
         if i < DEGREE - 1:
+            high, low = halves(base)
+            chosen = dot(picks[...], high) + dot(picks[...], low)
+            if i == 1:
+                greeted(greetings.at[0], reach + 1, min(2 * reach, n_grid - 1))
             wait_halo(i)
+            box = in_box[i].reshape(slots * halo, width)
+            passed = dot(passed_hi[...], box) + dot(passed_lo[...], box)
+            send_halo(i + 1, chosen + passed * gain[:1, :])
             outer_rows = base[INNER:] + far(i) * gain[:1, :]
             previous, current = current, jnp.concatenate([base[:INNER], outer_rows], axis=0)
-            send_halo(i + 1, current)
+            if i == 0:
+                greet(greetings.at[0], reach + 1, min(2 * reach, n_grid - 1))
             sigma_next = 1.0 / (twice_inverse - sigma)
             gain = 2.0 * sigma_next / half_width
             back = sigma * sigma_next
@@ -236,8 +282,17 @@
 
     for d in range(1, n_grid):
         share_out[d - 1] = share_of(lax.rem(g + d, n_grid)).astype(BF16)
-    for d in range(1, n_grid):
-        share_copy(d).start()
+    heard, known, turn = 2 * reach, 5 * reach, 1
+    while known < n_grid - 1:
+        final = min(known, n_grid - 1)
+        greet(greetings.at[turn], heard + 1, final)
+        greeted(greetings.at[turn], heard + 1, final)
+        heard, known, turn = known, 2 * known, turn + 1
+    upper_half = 2 * g >= n_grid
+    for order in range(n_grid - 1):
+        other = jnp.where(upper_half, order, n_grid - 1 - order)
+        skip = jnp.where(upper_half, jnp.where(other >= g, 1, 0), jnp.where(other <= g, -1, 0))
+        share_copy(lax.rem(other + skip - g + n_grid, n_grid)).start()
     result = share_of(g)
     for d in range(1, n_grid):
         share_copy(d).wait_recv()
@@ -310,6 +365,9 @@
             pltpu.VMEM((total_bands, total_bands), F32),
             pltpu.VMEM((n_grid - 1, per, total_bands), BF16),
             pltpu.VMEM((n_grid - 1, per, total_bands), BF16),
+            pltpu.SemaphoreType.REGULAR((n_grid,)),
+            pltpu.VMEM((slots * halo, slots * halo), BF16),
+            pltpu.VMEM((slots * halo, slots * halo), BF16),
             dma((DEGREE, slots)),
             dma((DEGREE, slots)),
             dma((2, n_band - 1)),

time: 26.4 us -> 26.1 us (0.989)
  Pallas kernels: 25 us -> 24.6 us
    pallas_call x1, Pallas kernels: 24.3 us -> 23.9 us  [on_device(): pl.pallas_call(functools.partial(kernel, n_grid, n_band), out_shape=tuple...]
where the time goes in v3:
time: 26.1 us; the launch traced here: 25.9 us
  Pallas kernels  24.6 us (94%)
  between operations  1.29 us (5%)
    pallas_call x1, Pallas kernels, on_device(): pl.pallas_call(functools.partial(kernel, n_grid, n_band), out_shape=tuple...  23.9 us
    pallas_call x1, Pallas kernels, on_device(): pl.pallas_call(finish, out_shape=outs, in_specs=[vmem, vmem], out_specs=(...  0.68 us

profile of v3, /device:TPU:0, one launch (start us, length us, event | category | flops | bytes accessed | tf_op | source)
XLA Modules:
  0.0 25.9 jit_solution(15656422632613681168)
XLA Ops:
  1.3 23.9 %shard_map.77 = (f32[256,128]{1,0:T(8,128)S(1)}, f32[8,256]{1,0:T(8,128)S(1)}) custom-call(f32[1,3]{1,0:T(1,128)} %bitcast.7, s32[1,1]{1,0:T(1,128)} %bitcast.4.count_hbm, f32[256,128]{1,0:T(8,128)} %states_hbm.1, f32[1,256]{1,0:T(1,128)} %bitcast.6, s32[6,1,64]{2,1,0:T(1,128)} %bitcast.5, s32[36,256]{1,0:T(8,128)} %table_hbm.1), custom_call_target="tpu_custom_call" | custom-call | tf_op jit(solution)/shard_map/pallas_call | solution.py:342
  25.2 0.7 %shard_map.78 = (f32[256,128]{1,0:T(8,128)}, f32[8,256]{1,0:T(8,128)}) custom-call(f32[256,128]{1,0:T(8,128)S(1)} %get-tuple-element.4.filtered, f32[8,256]{1,0:T(8,128)S(1)} %get-tuple-element.5.margin), custom_call_target="tpu_custom_call" | custom-call | tf_op jit(solution)/shard_map/pallas_call | solution.py:389
